TPU v7x, 8 devices: a whole 2x2x1 slice. The times are simulated.
8 devices in a mesh: dp: 1 (over z), tp: 8 (over y, x, core).
Axes of the slice: x: 2, y: 2, z: 1, core: 2. Of those that a mesh axis runs over, the one named last changes fastest.
Arguments:
- y_one: float32 [16, 32, 3072], P('dp')
- y_two: float32 [16, 32, 3072], P('dp')
- dy_one: float32 [16, 32, 3072], P('dp')
- dy_two: float32 [16, 32, 3072], P('dp')
- seq_lens: int32 [16], P('dp')
- w_query: bfloat16 [3, 3072, 24, 128], P(None, None, 'tp')
- w_key: bfloat16 [3, 3072, 8, 128], P(None, None, 'tp')
- w_value: bfloat16 [3, 3072, 8, 128], P(None, None, 'tp')
- w_out: bfloat16 [3, 24, 128, 3072], P(None, 'tp')
- w_up: bfloat16 [3, 3072, 8192], P(None, None, 'tp')
- w_down: bfloat16 [3, 8192, 3072], P(None, 'tp')
Outputs:
- output 1: float32 [16, 32, 3072], P('dp')
- output 2: float32 [16, 32, 3072], P('dp')
- output 3: float32 [16, 32, 3072], P('dp')
- output 4: float32 [16, 32, 3072], P('dp')
- output 5: float32 [3, 3072, 24, 128], P('dp', None, 'tp')
- output 6: float32 [3, 3072, 8, 128], P('dp', None, 'tp')
- output 7: float32 [3, 3072, 8, 128], P('dp', None, 'tp')
- output 8: float32 [3, 24, 128, 3072], P('dp', 'tp')
- output 9: float32 [3, 3072, 8192], P('dp', None, 'tp')
- output 10: float32 [3, 8192, 3072], P('dp', 'tp')
All inputs are finite; a program needn't handle non-finite values.
Results may differ from a plain program's by a relative error of at most 0.02.
Values are sent between devices in bfloat16 or wider.
A program may use at most 1 GiB of HBM per device.

v0:
```python
import jax
import jax.numpy as jnp
from jax import lax
from jax.sharding import PartitionSpec as P, NamedSharding

F32 = jnp.float32
BF16 = jnp.bfloat16
EPS = 1e-5
MASK_VALUE = -1e30


def rms_norm(x_val):
    inv_rms = lax.rsqrt(jnp.mean(x_val * x_val, axis=-1, keepdims=True) + EPS)
    return x_val * inv_rms, inv_rms


def rms_back(normed, inv_rms, grad_norm):
    return inv_rms * (grad_norm - normed * jnp.mean(grad_norm * normed, axis=-1, keepdims=True))


def visible_mask(seq_lens, seq_len):
    row_pos = lax.broadcasted_iota(jnp.int32, (seq_len, seq_len), 0)
    col_pos = lax.broadcasted_iota(jnp.int32, (seq_len, seq_len), 1)
    causal = (col_pos <= row_pos)[None, None, None]
    in_length = col_pos[None, None, None] < seq_lens[:, None, None, None, None]
    return causal & in_length


def block_back(carry, seq_lens, layer_w, all_reduce):
    y_one, y_two, dy_one, dy_two = carry
    w_query, w_key, w_value, w_out, w_up, w_down = layer_w
    n_batch, seq_len = y_one.shape[0], y_one.shape[1]
    n_heads, head_dim = w_query.shape[1], w_query.shape[2]
    kv_slots = w_key.shape[1]
    group_size = n_heads // kv_slots
    score_scale = head_dim ** -0.5

    norm_g, inv_g = rms_norm(y_one)
    norm_g_b = norm_g.astype(BF16)
    pre_act = jnp.einsum('bsd,df->bsf', norm_g_b, w_up, preferred_element_type=F32)
    act_val, gelu_back = jax.vjp(jax.nn.gelu, pre_act)
    act_b = act_val.astype(BF16)
    x_two = y_two - all_reduce(jnp.einsum('bsf,fd->bsd', act_b, w_down, preferred_element_type=F32))
    dy2_b = dy_two.astype(BF16)
    d_act = jnp.einsum('bsd,fd->bsf', dy2_b, w_down, preferred_element_type=F32)
    d_pre = gelu_back(d_act)[0].astype(BF16)
    dw_down = jnp.einsum('bsf,bsd->fd', act_b, dy2_b, preferred_element_type=F32)
    dw_up = jnp.einsum('bsd,bsf->df', norm_g_b, d_pre, preferred_element_type=F32)
    grad_norm_g = all_reduce(jnp.einsum('bsf,df->bsd', d_pre, w_up, preferred_element_type=F32))
    dy_one = dy_one + rms_back(norm_g, inv_g, grad_norm_g)

    norm_f, inv_f = rms_norm(x_two)
    norm_f_b = norm_f.astype(BF16)
    query_proj = jnp.einsum('bsd,dhe->bshe', norm_f_b, w_query, preferred_element_type=F32).astype(BF16)
    query_grp = query_proj.reshape(n_batch, seq_len, kv_slots, group_size, head_dim)
    key_proj = jnp.einsum('bsd,dge->bsge', norm_f_b, w_key, preferred_element_type=F32).astype(BF16)
    value_proj = jnp.einsum('bsd,dge->bsge', norm_f_b, w_value, preferred_element_type=F32).astype(BF16)
    scores = jnp.einsum('bigre,bjge->bgrij', query_grp, key_proj, preferred_element_type=F32) * score_scale
    scores = jnp.where(visible_mask(seq_lens, seq_len), scores, MASK_VALUE)
    attn_probs = jax.nn.softmax(scores, axis=-1)
    probs_b = attn_probs.astype(BF16)
    attn_out = jnp.einsum('bgrij,bjge->bigre', probs_b, value_proj, preferred_element_type=F32).astype(BF16)
    attn_out = attn_out.reshape(n_batch, seq_len, n_heads, head_dim)
    x_one = y_one - all_reduce(jnp.einsum('bihe,hed->bid', attn_out, w_out, preferred_element_type=F32))
    dy1_b = dy_one.astype(BF16)
    dw_out = jnp.einsum('bihe,bid->hed', attn_out, dy1_b, preferred_element_type=F32)
    d_attn = jnp.einsum('bid,hed->bihe', dy1_b, w_out, preferred_element_type=F32).astype(BF16)
    d_attn = d_attn.reshape(n_batch, seq_len, kv_slots, group_size, head_dim)
    d_value = jnp.einsum('bgrij,bigre->bjge', probs_b, d_attn, preferred_element_type=F32).astype(BF16)
    d_probs = jnp.einsum('bigre,bjge->bgrij', d_attn, value_proj, preferred_element_type=F32)
    d_scores = (attn_probs * (d_probs - jnp.sum(d_probs * attn_probs, axis=-1, keepdims=True)) * score_scale).astype(BF16)
    d_query = jnp.einsum('bgrij,bjge->bigre', d_scores, key_proj, preferred_element_type=F32).astype(BF16)
    d_query = d_query.reshape(n_batch, seq_len, n_heads, head_dim)
    d_key = jnp.einsum('bgrij,bigre->bjge', d_scores, query_grp, preferred_element_type=F32).astype(BF16)
    dw_query = jnp.einsum('bsd,bshe->dhe', norm_f_b, d_query, preferred_element_type=F32)
    dw_key = jnp.einsum('bsd,bsge->dge', norm_f_b, d_key, preferred_element_type=F32)
    dw_value = jnp.einsum('bsd,bsge->dge', norm_f_b, d_value, preferred_element_type=F32)
    grad_norm_f = all_reduce(jnp.einsum('bshe,dhe->bsd', d_query, w_query, preferred_element_type=F32)
                             + jnp.einsum('bsge,dge->bsd', d_key, w_key, preferred_element_type=F32)
                             + jnp.einsum('bsge,dge->bsd', d_value, w_value, preferred_element_type=F32))
    dx_two = dy_two + rms_back(norm_f, inv_f, grad_norm_f)
    return (x_one, x_two, dy_one, dx_two), (dw_query, dw_key, dw_value, dw_out, dw_up, dw_down)


def stack_grads(grads_by_layer):
    return tuple(jnp.stack([layer_grads[grad_pos] for layer_grads in grads_by_layer]) for grad_pos in range(6))


def tp_sum(partial_val):
    return lax.psum(partial_val, 'tp')


def solution(mesh):
    act_spec = P('dp', None, None)
    w_specs = (P(None, None, 'tp', None), P(None, None, 'tp', None), P(None, None, 'tp', None),
               P(None, 'tp', None, None), P(None, None, 'tp'), P(None, 'tp', None))
    g_specs = (P('dp', None, 'tp', None), P('dp', None, 'tp', None), P('dp', None, 'tp', None),
               P('dp', 'tp', None, None), P('dp', None, 'tp'), P('dp', 'tp', None))

    def local_fn(y_one, y_two, dy_one, dy_two, seq_lens, w_query, w_key, w_value, w_out, w_up, w_down):
        weights = (w_query, w_key, w_value, w_out, w_up, w_down)
        carry = (y_one, y_two, dy_one, dy_two)
        n_layers = w_query.shape[0]
        grads_by_layer = [None] * n_layers
        for layer_idx in reversed(range(n_layers)):
            layer_w = tuple(w_stack[layer_idx] for w_stack in weights)
            carry, grads_by_layer[layer_idx] = block_back(carry, seq_lens, layer_w, tp_sum)
        return carry + stack_grads(grads_by_layer)

    return jax.shard_map(local_fn, mesh=mesh,
                         in_specs=(act_spec,) * 4 + (P('dp'),) + w_specs,
                         out_specs=(act_spec,) * 4 + g_specs,
                         check_vma=False)
```

profile of v0, /device:TPU:0, one launch (start us, length us, event | category | flops | bytes accessed | tf_op | source)
XLA Modules:
  0.0 1324.7 jit_solution(12015338495627471091)
XLA Ops:
  17.6 9.0 fusion.21
  43.9 162.6 %all-reduce.23.cloned.1.call-done = (f32[16,32,3072]{2,1,0:T(8,128)}, f32[16,32,3072]{2,1,0:T(8,128)}) async-done(((f32[16,32,3072]{2,1,0:T(8,128)}, f32[16,32,3072]{2,1,0:T(8,128)}), (f32[16,32,3072]{2,1,0:T(8,128)}, f32[16,32,3072]{2,1,0:T(8,128)})) %all-reduce.23.cloned.1.call-update) | async-done | bytes 12582928 | tf_op jit(solution)/shard_map/psum | solution.py:90
  211.9 14.8 %multiply_reduce_fusion.10 = (f32[16,32]{1,0:T(8,128)S(1)}, f32[16,32,3072]{2,1,0:T(8,128)S(1)}, f32[16,32,3072]{2,1,0:T(8,128)}) fusion(f32[16,32,3072]{2,1,0:T(8,128)} %param.12, f32[16,32,3072]{2,1,0:T(8,128)} %get-tuple-element.30, f32[16,32,3072]{2,1,0:T(8,128)} %param.13, f32[16,32,3072]{2,1,0:T(8,128)} %get-tuple-element.31, ...), kind=kLoop, calls=%fused_computation.56 | loop fusion | flops 12582400 | bytes 44046336 | tf_op jit(solution)/shard_map/reduce_sum | solution.py:13
  255.0 160.6 %all-reduce.21.cloned.1.call-done = (f32[16,32,3072]{2,1,0:T(8,128)}, f32[16,32,3072]{2,1,0:T(8,128)}) async-done(((f32[16,32,3072]{2,1,0:T(8,128)}, f32[16,32,3072]{2,1,0:T(8,128)}), (f32[16,32,3072]{2,1,0:T(8,128)}, f32[16,32,3072]{2,1,0:T(8,128)})) %all-reduce.21.cloned.1.call-update) | async-done | bytes 12582928 | tf_op jit(solution)/shard_map/psum | solution.py:90
  421.0 12.0 multiply_add_fusion.4
  438.6 15.3 %fusion.17 = f32[16,32,1024]{2,1,0:T(8,128)S(1)} fusion(bf16[3,3072,1024]{2,1,0:T(8,128)(2,1)} %param.20, f32[16,32,3072]{2,1,0:T(8,128)S(1)} %get-tuple-element.39, f32[16,32]{1,0:T(8,128)S(1)} %add_rsqrt_fusion.3), kind=kOutput, calls=%fused_computation.30 | convolution fusion | flops 3224371200 | bytes 14682112 | tf_op jit(solution)/shard_map/bsd,df->bsf/dot_general | solution.py:40
  453.9 9.0 fusion.13
  479.6 11.5 convolution_bitcast_fusion.3
  491.2 9.9 convolution_bitcast_fusion
  510.9 129.4 %all-reduce.19.cloned.1.call-done = (f32[16,32,3072]{2,1,0:T(8,128)}, f32[16,32,3072]{2,1,0:T(8,128)}) async-done(((f32[16,32,3072]{2,1,0:T(8,128)}, f32[16,32,3072]{2,1,0:T(8,128)}), (f32[16,32,3072]{2,1,0:T(8,128)}, f32[16,32,3072]{2,1,0:T(8,128)})) %all-reduce.19.cloned.1.call-update) | async-done | bytes 12582928 | tf_op jit(solution)/shard_map/psum | solution.py:90
  660.0 12.0 multiply_add_fusion.3
  701.8 9.8 convolution_bitcast_fusion.4
  724.4 133.0 %all-reduce.17.cloned.1.call-done = (f32[16,32,3072]{2,1,0:T(8,128)}, f32[16,32,3072]{2,1,0:T(8,128)}) async-done(((f32[16,32,3072]{2,1,0:T(8,128)}, f32[16,32,3072]{2,1,0:T(8,128)}), (f32[16,32,3072]{2,1,0:T(8,128)}, f32[16,32,3072]{2,1,0:T(8,128)})) %all-reduce.17.cloned.1.call-update) | async-done | bytes 12582928 | tf_op jit(solution)/shard_map/psum | solution.py:90
  862.8 12.0 multiply_add_fusion.2
  888.1 9.0 fusion.5
  934.5 139.8 %all-reduce.15.cloned.1.call-done = (f32[16,32,3072]{2,1,0:T(8,128)}, f32[16,32,3072]{2,1,0:T(8,128)}) async-done(((f32[16,32,3072]{2,1,0:T(8,128)}, f32[16,32,3072]{2,1,0:T(8,128)}), (f32[16,32,3072]{2,1,0:T(8,128)}, f32[16,32,3072]{2,1,0:T(8,128)})) %all-reduce.15.cloned.1.call-update) | async-done | bytes 12582928 | tf_op jit(solution)/shard_map/psum | solution.py:90
  1092.6 12.2 multiply_add_fusion.1
  1130.5 28.4 %pad_maximum_fusion.1 = f32[3,1024,3072]{2,1,0:T(8,128)} fusion(f32[1,1024,3072]{2,1,0:T(8,128)} %convolution_bitcast_fusion, f32[1,1024,3072]{2,1,0:T(8,128)} %convolution_bitcast_fusion.1, f32[1,1024,3072]{2,1,0:T(8,128)} %convolution_bitcast_fusion.2), kind=kLoop, calls=%fused_computation.1 | loop fusion | flops 18874368 | bytes 75497472 | tf_op jit(solution)/shard_map/stack | solution.py:86
  1158.9 28.5 %pad_maximum_fusion = f32[3,3072,1024]{2,1,0:T(8,128)} fusion(f32[1,3072,1024]{2,1,0:T(8,128)} %convolution_bitcast_fusion.3, f32[1,3072,1024]{2,1,0:T(8,128)} %convolution_bitcast_fusion.4, f32[1,3072,1024]{2,1,0:T(8,128)} %convolution_bitcast_fusion.5), kind=kLoop, calls=%fused_computation | loop fusion | flops 18874368 | bytes 75497472 | tf_op jit(solution)/shard_map/stack | solution.py:86
  1200.2 12.5 pad_maximum_fusion.3
  1216.7 11.3 pad_maximum_fusion.2
  1228.0 63.1 %all-reduce.13.cloned.1.call-done = (f32[16,32,3072]{2,1,0:T(8,128)}, f32[16,32,3072]{2,1,0:T(8,128)}) async-done(((f32[16,32,3072]{2,1,0:T(8,128)}, f32[16,32,3072]{2,1,0:T(8,128)}), (f32[16,32,3072]{2,1,0:T(8,128)}, f32[16,32,3072]{2,1,0:T(8,128)})) %all-reduce.13.cloned.1.call-update) | async-done | bytes 12582928 | tf_op jit(solution)/shard_map/psum | solution.py:90
  1296.5 12.0 multiply_add_fusion
  1308.6 8.9 sub.104
  (296 shorter events, 282.2 us)
Async XLA Ops:
  7.2 199.4 %all-reduce.23.cloned.1.call-start = ((), (), s32[]{:S(2)}) async-start(), calls=%async_computation.5 | async-start | bytes 25165824 | tf_op jit(solution)/shard_map/psum | solution.py:90
  7.2 19.4 %slice-start.26 = ((s8[6291456]{0:T(1024)(128)(4,1)}), s8[4194304]{0:T(1024)(128)(4,1)S(1)}, s32[]{:S(2)}) async-start(s8[6291456]{0:T(1024)(128)(4,1)} %bitcast.574), calls=%async_computation.32 | async-start | bytes 8388608
  11.8 14.9 %slice-start.27 = ((s8[6291456]{0:T(1024)(128)(4,1)}), s8[2097152]{0:T(1024)(128)(4,1)S(1)}, s32[]{:S(2)}) async-start(s8[6291456]{0:T(1024)(128)(4,1)} %bitcast.574), calls=%async_computation.33 | async-start | bytes 4194304
  43.2 372.5 %all-reduce.21.cloned.1.call-start = ((), (), s32[]{:S(2)}) async-start(), calls=%async_computation.4 | async-start | bytes 25165824 | tf_op jit(solution)/shard_map/psum | solution.py:90
  43.9 194.1 %copy-start.16 = (pred[16,32,32]{1,2,0:T(8,128)(4,1)}, pred[16,32,32]{1,2,0:T(8,128)(4,1)S(1)}, u32[]{:S(2)}) copy-start(pred[16,32,32]{1,2,0:T(8,128)(4,1)S(1)} %fusion.225) | copy-start | bytes 49156
  229.9 277.0 %copy-start.6 = (bf16[16,32,3072]{2,1,0:T(8,128)(2,1)}, bf16[16,32,3072]{2,1,0:T(8,128)(2,1)S(1)}, u32[]{:S(2)}) copy-start(bf16[16,32,3072]{2,1,0:T(8,128)(2,1)S(1)} %multiply_convert_fusion.4) | copy-start | bytes 9437188
  255.0 385.3 %all-reduce.19.cloned.1.call-start = ((), (), s32[]{:S(2)}) async-start(), calls=%async_computation.3 | async-start | bytes 25165824 | tf_op jit(solution)/shard_map/psum | solution.py:90
  433.1 29.9 %slice-start.22 = ((s8[6291456]{0:T(1024)(128)(4,1)}), s8[4194304]{0:T(1024)(128)(4,1)S(1)}, s32[]{:S(2)}) async-start(s8[6291456]{0:T(1024)(128)(4,1)} %bitcast.570), calls=%async_computation.28 | async-start | bytes 8388608
  438.6 15.3 %copy-start.4 = (f32[16,32,3072]{2,1,0:T(8,128)}, f32[16,32,3072]{2,1,0:T(8,128)S(1)}, u32[]{:S(2)}) copy-start(f32[16,32,3072]{2,1,0:T(8,128)S(1)} %get-tuple-element.39) | copy-start | bytes 18874372
  438.6 15.3 %copy-start.38 = (f32[16,32]{1,0:T(8,128)}, f32[16,32]{1,0:T(8,128)S(1)}, u32[]{:S(2)}) copy-start(f32[16,32]{1,0:T(8,128)S(1)} %add_rsqrt_fusion.3) | copy-start | bytes 6148
  438.6 24.4 %slice-start.23 = ((s8[6291456]{0:T(1024)(128)(4,1)}), s8[2097152]{0:T(1024)(128)(4,1)S(1)}, s32[]{:S(2)}) async-start(s8[6291456]{0:T(1024)(128)(4,1)} %bitcast.570), calls=%async_computation.29 | async-start | bytes 4194304
  479.6 377.8 %all-reduce.17.cloned.1.call-start = ((), (), s32[]{:S(2)}) async-start(), calls=%async_computation.2 | async-start | bytes 25165824 | tf_op jit(solution)/shard_map/psum | solution.py:90
  479.6 23.6 %slice-start.10 = ((s8[6291456]{0:T(1024)(128)(4,1)}), s8[4194304]{0:T(1024)(128)(4,1)S(1)}, s32[]{:S(2)}) async-start(s8[6291456]{0:T(1024)(128)(4,1)} %bitcast.558), calls=%async_computation.16 | async-start | bytes 8388608
  645.6 13.5 %slice-start.4 = ((s8[6291456]{0:T(1024)(128)(4,1)}), s8[4194304]{0:T(1024)(128)(4,1)S(1)}, s32[]{:S(2)}) async-start(s8[6291456]{0:T(1024)(128)(4,1)} %bitcast.552), calls=%async_computation.10 | async-start | bytes 8388608
  645.6 13.5 %slice-start.14 = ((s8[6291456]{0:T(1024)(128)(4,1)}), s8[4194304]{0:T(1024)(128)(4,1)S(1)}, s32[]{:S(2)}) async-start(s8[6291456]{0:T(1024)(128)(4,1)} %bitcast.562), calls=%async_computation.20 | async-start | bytes 8388608
  696.7 377.6 %all-reduce.15.cloned.1.call-start = ((), (), s32[]{:S(2)}) async-start(), calls=%async_computation.1 | async-start | bytes 25165824 | tf_op jit(solution)/shard_map/psum | solution.py:90
  701.8 18.9 %slice-start.6 = ((s8[6291456]{0:T(1024)(128)(4,1)}), s8[4194304]{0:T(1024)(128)(4,1)S(1)}, s32[]{:S(2)}) async-start(s8[6291456]{0:T(1024)(128)(4,1)} %bitcast.554), calls=%async_computation.12 | async-start | bytes 8388608
  874.7 22.4 %slice-start.18 = ((s8[6291456]{0:T(1024)(128)(4,1)}), s8[4194304]{0:T(1024)(128)(4,1)S(1)}, s32[]{:S(2)}) async-start(s8[6291456]{0:T(1024)(128)(4,1)} %bitcast.566), calls=%async_computation.24 | async-start | bytes 8388608
  880.2 16.9 %slice-start.19 = ((s8[6291456]{0:T(1024)(128)(4,1)}), s8[2097152]{0:T(1024)(128)(4,1)S(1)}, s32[]{:S(2)}) async-start(s8[6291456]{0:T(1024)(128)(4,1)} %bitcast.566), calls=%async_computation.25 | async-start | bytes 4194304
  913.6 377.5 %all-reduce.13.cloned.1.call-start = ((), (), s32[]{:S(2)}) async-start(), calls=%async_computation | async-start | bytes 25165824 | tf_op jit(solution)/shard_map/psum | solution.py:90
  1091.5 19.5 %copy-start.42 = (bf16[16,32,128,1]{2,1,3,0:T(8,128)(2,1)}, bf16[16,32,128,1]{2,1,3,0:T(8,128)(2,1)S(1)}, u32[]{:S(2)}) copy-start(bf16[16,32,128,1]{2,1,3,0:T(8,128)(2,1)S(1)} %fusion.181) | copy-start | bytes 393220
  1111.7 13.9 %copy-start.34 = (bf16[16,32,128]{2,1,0:T(8,128)(2,1)}, bf16[16,32,128]{2,1,0:T(8,128)(2,1)S(1)}, u32[]{:S(2)}) copy-start(bf16[16,32,128]{2,1,0:T(8,128)(2,1)S(1)} %fusion.171) | copy-start | bytes 393220
  1158.9 28.5 %copy-start.35 = (bf16[16,32,128]{2,1,0:T(8,128)(2,1)S(1)}, bf16[16,32,128]{2,1,0:T(8,128)(2,1)}, u32[]{:S(2)}) copy-start(bf16[16,32,128]{2,1,0:T(8,128)(2,1)} %copy-done.34) | copy-start | bytes 393220
  1216.7 74.4 %copy-start.37 = (f32[16,32]{1,0:T(8,128)S(1)}, f32[16,32]{1,0:T(8,128)}, u32[]{:S(2)}) copy-start(f32[16,32]{1,0:T(8,128)} %copy-done.36) | copy-start | bytes 6148
  (66 other events, 418.6 us)
Sparse Core Ops, SparseCore 0:
  43.3 163.2 all-reduce.22
  255.1 160.5 all-reduce.20
  479.7 160.5 all-reduce.18
  696.8 160.5 all-reduce.16
  913.8 160.5 all-reduce.14
  1130.6 160.5 all-reduce.12
where the time goes:
time: 1330 us; the launch traced here: 1320 us
  waiting for transfers between devices  789 us (59%)
  matrix products  281 us (21%)
  other arithmetic  223 us (17%)
  local copies, waits for them, and re-layouts  16.8 us (1%)
  between operations  15.6 us (1%)
    psum x6, waiting for transfers between devices, tp_sum(): return lax.psum(partial_val, 'tp')  789 us
    another operation x6, other arithmetic, stack_grads(): jnp.stack([layer_grads[grad_pos] for layer_grads in grads_by_layer])  85.9 us
    reduce_sum x6, other arithmetic, rms_norm(): inv_rms = lax.rsqrt(jnp.mean(x_val * x_val, axis=-1, keepdims=True) + EPS)  39.9 us
    add x3, other arithmetic, block_back(): dx_two = dy_two + rms_back(norm_f, inv_f, grad_norm_f)  36 us
    dot_general x3, matrix products, block_back(): jnp.einsum('bsd,df->bsf', norm_g_b, w_up, preferred_element_type=F32)  29 us
    dot_general x3, matrix products, block_back(): jnp.einsum('bsd,bsf->df', norm_g_b, d_pre, preferred_element_type=F32)  28 us
    dot_general x3, matrix products, block_back(): jnp.einsum('bsf,fd->bsd', act_b, w_down, preferred_element_type=F32)  27.1 us
  transfers between devices with their start and end apart: 6, of which 6 were waited for; matrix products, arithmetic and copies ran while one was open for 13% of the time, Pallas kernels for 0%

commit v1 on v0

v1 whole, which is shorter than its diff:
```python
import functools

import jax
import jax.numpy as jnp
from jax import lax
from jax.experimental import pallas as pl
from jax.experimental.pallas import tpu as pltpu
from jax.sharding import PartitionSpec as P

F32 = jnp.float32
BF16 = jnp.bfloat16
EPS = 1e-5
MASK_VALUE = -1e30
MESH = pl.DeviceIdType.MESH
TILE = 128
N_TILES = 4
GELU_C = 0.7978845608028654
GELU_A = 0.044715
OWNER = (0, 4, 2, 6, 1, 3, 5, 7)
ORDER = (('e', 3), ('g', 4), ('C', 0), ('f', 3), ('b', 0), ('c', 1), ('d', 2))


def dot_nn(lhs, rhs):
    return lax.dot_general(lhs, rhs, (((1,), (0,)), ((), ())), preferred_element_type=F32)


def dot_nt(lhs, rhs):
    return lax.dot_general(lhs, rhs, (((1,), (1,)), ((), ())), preferred_element_type=F32)


def dot_tn(lhs, rhs):
    return lax.dot_general(lhs, rhs, (((0,), (0,)), ((), ())), preferred_element_type=F32)


def inv_rms_of(x_val):
    return lax.rsqrt(jnp.mean(x_val * x_val, axis=-1, keepdims=True) + EPS)


def stack_kernel(n_layers, width, ff, qw, kw,
                 ne0, mask, y_one, y_two, dy_one, dy_two, w_qkv, w_out, w_up, w_down,
                 o_state, o_ng, o_eg, o_h, o_u, o_nf, o_ef, o_a, o_dq, o_dk, o_dv,
                 ne, part, rec_d, rec_one, rec_two, x_st, d_st, wu, wd, wqkv, wo, h_buf, u_buf,
                 a_buf, dqkv_buf, q_buf, send_sem, recv_sem, w_sem, in_sem, out_sem):
    n_steps = 2 * n_layers * N_TILES
    me = lax.axis_index('tp')
    core = me % 2
    x_pos = (me // 2) % 2
    y_pos = me // 4
    mate = me + 1 - 2 * core
    x_peer = me + 2 - 4 * x_pos
    y_peer = me + 4 - 8 * y_pos
    peer_one = x_peer * (1 - core) + y_peer * core
    peer_two = y_peer * (1 - core) + x_peer * core
    bit_one = x_pos * (1 - core) + y_pos * core
    bit_two = y_pos * (1 - core) + x_pos * core
    half = pl.multiple_of(core * 64, 64)
    half_other = pl.multiple_of(64 - core * 64, 64)
    quarter = pl.multiple_of(half + bit_one * 32, 32)
    quarter_other = pl.multiple_of(half + 32 - bit_one * 32, 32)
    own = pl.multiple_of(quarter + bit_two * 16, 16)
    own_other = pl.multiple_of(quarter + 16 - bit_two * 16, 16)

    def mlp_loads(layer):
        return (pltpu.make_async_copy(w_up.at[layer], wu, w_sem.at[0]),
                pltpu.make_async_copy(w_down.at[layer], wd, w_sem.at[1]))

    def attn_loads(layer):
        return (pltpu.make_async_copy(w_qkv.at[layer], wqkv, w_sem.at[2]),
                pltpu.make_async_copy(w_out.at[layer], wo, w_sem.at[3]))

    in_copies = [pltpu.make_async_copy(ne0, ne, in_sem.at[0])]
    for pos, (src, dst) in enumerate(((y_one, x_st.at[0]), (y_two, x_st.at[1]),
                                      (dy_one, d_st.at[0]), (dy_two, d_st.at[1]))):
        for tile in range(N_TILES):
            in_copies.append(pltpu.make_async_copy(
                src.at[pl.ds(tile * TILE + own, 16), :], dst.at[tile], in_sem.at[1 + pos * N_TILES + tile]))
    for copy in mlp_loads(n_layers - 1):
        copy.start()
    for copy in in_copies:
        copy.start()
    for copy in attn_loads(n_layers - 1):
        copy.start()

    barrier = pltpu.get_barrier_semaphore()
    for peer in (mate, x_peer, y_peer):
        pl.semaphore_signal(barrier, inc=1, device_id={'tp': peer}, device_id_type=MESH)
    pl.semaphore_wait(barrier, 3)
    for copy in in_copies:
        copy.wait()

    def remote(stage, tile):
        src, dst, peer = {
            0: lambda: (part.at[tile, :, pl.ds(half_other, 64), :], rec_d.at[tile], mate),
            1: lambda: (part.at[tile, :, pl.ds(quarter_other, 32), :], rec_one.at[tile], peer_one),
            2: lambda: (part.at[tile, :, pl.ds(own_other, 16), :], rec_two.at[tile], peer_two),
            3: lambda: (ne.at[tile, :, pl.ds(own, 16), :], ne.at[tile, :, pl.ds(own, 16), :], peer_two),
            4: lambda: (ne.at[tile, :, pl.ds(quarter, 32), :], ne.at[tile, :, pl.ds(quarter, 32), :], peer_one),
            5: lambda: (ne.at[tile, :, pl.ds(half, 64), :], ne.at[tile, :, pl.ds(half, 64), :], mate),
        }[stage]()
        return pltpu.make_async_remote_copy(
            src_ref=src, dst_ref=dst, send_sem=send_sem.at[tile, stage], recv_sem=recv_sem.at[tile, stage],
            device_id={'tp': peer}, device_id_type=MESH)

    def mlp_tile(layer, tile):
        rows = pl.ds(tile * TILE, TILE)
        saves = [pltpu.make_async_copy(ne.at[tile, 0], o_ng.at[layer, rows, :], out_sem.at[0]),
                 pltpu.make_async_copy(ne.at[tile, 1], o_eg.at[layer, rows, :], out_sem.at[1])]
        for copy in saves:
            copy.start()

        @pl.when(tile == 0)
        def _():
            for copy in mlp_loads(layer):
                copy.wait()

        @pl.loop(0, ff // 256)
        def _(pos):
            cols = pl.ds(pl.multiple_of(pos * 256, 256), 256)
            pre = dot_nn(ne[tile, 0], wu[:, cols])
            d_act = dot_nt(ne[tile, 1], wd[cols, :])
            tanh_val = jnp.tanh(GELU_C * (pre + GELU_A * (pre * pre * pre)))
            h_buf[:, cols] = (0.5 * pre * (1.0 + tanh_val)).astype(BF16)
            slope = 0.5 * (1.0 + tanh_val) + (0.5 * GELU_C) * pre * (1.0 - tanh_val * tanh_val) * (1.0 + (3.0 * GELU_A) * (pre * pre))
            u_buf[:, cols] = (slope * d_act).astype(BF16)

        more = [pltpu.make_async_copy(h_buf, o_h.at[layer, rows, :], out_sem.at[2]),
                pltpu.make_async_copy(u_buf, o_u.at[layer, rows, :], out_sem.at[3])]
        for copy in more:
            copy.start()

        @pl.loop(0, width // 512)
        def _(pos):
            cols = pl.ds(pl.multiple_of(pos * 512, 512), 512)
            part[tile, 0, :, cols] = dot_nn(h_buf[...], wd[:, cols])
            part[tile, 1, :, cols] = dot_nt(u_buf[...], wu[cols, :])

        for copy in saves + more:
            copy.wait()

        @pl.when((tile == N_TILES - 1) & (layer > 0))
        def _():
            for copy in mlp_loads(layer - 1):
                copy.start()

    def attn_tile(layer, tile):
        rows = pl.ds(tile * TILE, TILE)
        saves = [pltpu.make_async_copy(ne.at[tile, 0], o_nf.at[layer, rows, :], out_sem.at[0]),
                 pltpu.make_async_copy(ne.at[tile, 1], o_ef.at[layer, rows, :], out_sem.at[1])]
        for copy in saves:
            copy.start()

        @pl.when(tile == 0)
        def _():
            for copy in attn_loads(layer):
                copy.wait()

        n_val = ne[tile, 0]
        q_buf[:, :qw] = dot_nn(n_val, wqkv[:, :qw]).astype(BF16)
        q_buf[:, qw:] = dot_nn(n_val, wqkv[:, qw:]).astype(BF16)
        key = q_buf[:, qw:qw + kw]
        value = q_buf[:, qw + kw:]
        d_attn_all = dot_nt(ne[tile, 1], wo[...]).astype(BF16)
        visible = mask[tile] > 0.5
        scale = kw ** -0.5
        d_key = jnp.zeros((TILE, kw), F32)
        d_value = jnp.zeros((TILE, kw), F32)
        for head in range(qw // kw):
            cols = slice(head * kw, (head + 1) * kw)
            query = q_buf[:, cols]
            d_attn = d_attn_all[:, cols]
            scores = jnp.where(visible, dot_nt(query, key) * scale, MASK_VALUE)
            weights = jnp.exp(scores - jnp.max(scores, axis=-1, keepdims=True))
            probs = weights / jnp.sum(weights, axis=-1, keepdims=True)
            probs_b = probs.astype(BF16)
            a_buf[:, cols] = dot_nn(probs_b, value).astype(BF16)
            d_value += dot_tn(probs_b, d_attn)
            d_probs = dot_nt(d_attn, value)
            d_scores = (probs * (d_probs - jnp.sum(d_probs * probs, axis=-1, keepdims=True)) * scale).astype(BF16)
            dqkv_buf[:, cols] = dot_nn(d_scores, key).astype(BF16)
            d_key += dot_tn(d_scores, query)
        dqkv_buf[:, qw:qw + kw] = d_key.astype(BF16)
        dqkv_buf[:, qw + kw:] = d_value.astype(BF16)

        more = [pltpu.make_async_copy(a_buf, o_a.at[layer, rows, :], out_sem.at[2]),
                pltpu.make_async_copy(dqkv_buf.at[:, :qw], o_dq.at[layer, rows, :], out_sem.at[3]),
                pltpu.make_async_copy(dqkv_buf.at[:, qw:qw + kw], o_dk.at[layer, rows, :], out_sem.at[4]),
                pltpu.make_async_copy(dqkv_buf.at[:, qw + kw:], o_dv.at[layer, rows, :], out_sem.at[5])]
        for copy in more:
            copy.start()

        @pl.loop(0, width // 512)
        def _(pos):
            cols = pl.ds(pl.multiple_of(pos * 512, 512), 512)
            part[tile, 0, :, cols] = dot_nn(a_buf[...], wo[:, cols])
            part[tile, 1, :, cols] = dot_nt(dqkv_buf[...], wqkv[cols, :])

        for copy in saves + more:
            copy.wait()

        @pl.when((tile == N_TILES - 1) & (layer > 0))
        def _():
            for copy in attn_loads(layer - 1):
                copy.start()

    def add_rows(tile, base, n_rows, received):
        for unit in range(2):
            @pl.loop(0, n_rows // 8)
            def _(pos):
                row = pl.multiple_of(pos * 8, 8)
                dst = pl.ds(pl.multiple_of(base + row, 8), 8)
                part[tile, unit, dst, :] += received[tile, unit, pl.ds(row, 8), :]

    def finish_rows(branch, tile):
        rows = pl.ds(own, 16)
        other = 1 - branch
        x_new = x_st[other, tile] - (part[tile, 0, rows, :] + rec_two[tile, 0])
        x_st[other, tile] = x_new
        ne[tile, 0, rows, :] = (x_new * inv_rms_of(x_new)).astype(BF16)
        grad = part[tile, 1, rows, :] + rec_two[tile, 1]
        x_val = x_st[branch, tile]
        inv = inv_rms_of(x_val)
        normed = x_val * inv
        d_new = d_st[branch, tile] + inv * (grad - normed * jnp.mean(grad * normed, axis=-1, keepdims=True))
        d_st[branch, tile] = d_new
        ne[tile, 1, rows, :] = d_new.astype(BF16)

    def run_stage(stage, idx):
        tile = idx % N_TILES
        turn = idx // N_TILES
        branch = turn % 2
        layer = n_layers - 1 - turn // 2
        travels = idx < n_steps - N_TILES
        if stage == 'C':
            @pl.when(branch == 0)
            def _():
                mlp_tile(layer, tile)

            @pl.when(branch == 1)
            def _():
                attn_tile(layer, tile)
            remote(0, tile).start()
        elif stage == 'b':
            remote(0, tile).wait()
            add_rows(tile, half, 64, rec_d)
            remote(1, tile).start()
        elif stage == 'c':
            remote(1, tile).wait()
            add_rows(tile, quarter, 32, rec_one)
            remote(2, tile).start()
        elif stage == 'd':
            remote(2, tile).wait()
            finish_rows(branch, tile)

            @pl.when(travels)
            def _():
                remote(3, tile).start()
        elif stage == 'e':
            @pl.when(travels)
            def _():
                remote(3, tile).wait()
                remote(4, tile).start()
        elif stage == 'f':
            @pl.when(travels)
            def _():
                remote(4, tile).wait()
                remote(5, tile).start()
        else:
            @pl.when(travels)
            def _():
                remote(5, tile).wait()

    max_lag = max(lag for _, lag in ORDER)

    @pl.loop(0, n_steps + max_lag)
    def _(step):
        for stage, lag in ORDER:
            @pl.when((step >= lag) & (step < n_steps + lag))
            def _():
                run_stage(stage, step - lag)

    finals = []
    for pos, src in enumerate((x_st.at[0], x_st.at[1], d_st.at[0], d_st.at[1])):
        finals.append(pltpu.make_async_copy(src, o_state.at[pos], out_sem.at[pos]))
    for copy in finals:
        copy.start()
    for copy in finals:
        copy.wait()


def run_stack(ne0, mask, y_one, y_two, dy_one, dy_two, w_qkv, w_out, w_up, w_down):
    n_layers, width, ff = w_up.shape
    qw = w_out.shape[1]
    kw = (w_qkv.shape[2] - qw) // 2
    tokens = y_one.shape[0]
    any_spec = pl.BlockSpec(memory_space=pl.ANY)
    out = lambda *shape: jax.ShapeDtypeStruct((n_layers, tokens) + shape, BF16)
    return pl.pallas_call(
        functools.partial(stack_kernel, n_layers, width, ff, qw, kw),
        out_shape=(jax.ShapeDtypeStruct((4, N_TILES, 16, width), F32),
                   out(width), out(width), out(ff), out(ff), out(width), out(width),
                   out(qw), out(qw), out(kw), out(kw)),
        in_specs=[any_spec, pl.BlockSpec(memory_space=pltpu.VMEM)] + [any_spec] * 8,
        out_specs=(any_spec,) * 11,
        scratch_shapes=[
            pltpu.VMEM((N_TILES, 2, TILE, width), BF16),
            pltpu.VMEM((N_TILES, 2, TILE, width), F32),
            pltpu.VMEM((N_TILES, 2, 64, width), F32),
            pltpu.VMEM((N_TILES, 2, 32, width), F32),
            pltpu.VMEM((N_TILES, 2, 16, width), F32),
            pltpu.VMEM((2, N_TILES, 16, width), F32),
            pltpu.VMEM((2, N_TILES, 16, width), F32),
            pltpu.VMEM((width, ff), BF16),
            pltpu.VMEM((ff, width), BF16),
            pltpu.VMEM((width, qw + 2 * kw), BF16),
            pltpu.VMEM((qw, width), BF16),
            pltpu.VMEM((TILE, ff), BF16),
            pltpu.VMEM((TILE, ff), BF16),
            pltpu.VMEM((TILE, qw), BF16),
            pltpu.VMEM((TILE, qw + 2 * kw), BF16),
            pltpu.VMEM((TILE, qw + 2 * kw), BF16),
            pltpu.SemaphoreType.DMA((N_TILES, 6)),
            pltpu.SemaphoreType.DMA((N_TILES, 6)),
            pltpu.SemaphoreType.DMA((4,)),
            pltpu.SemaphoreType.DMA((1 + 4 * N_TILES,)),
            pltpu.SemaphoreType.DMA((6,)),
        ],
        compiler_params=pltpu.CompilerParams(
            collective_id=0, has_side_effects=True, vmem_limit_bytes=67043328),
        name='stack',
    )(ne0, mask, y_one, y_two, dy_one, dy_two, w_qkv, w_out, w_up, w_down)


def tile_mask(seq_lens, seq_len):
    n_seq = TILE // seq_len
    row = lax.broadcasted_iota(jnp.int32, (N_TILES, TILE, TILE), 1)
    col = lax.broadcasted_iota(jnp.int32, (N_TILES, TILE, TILE), 2)
    lens = jnp.repeat(seq_lens.reshape(N_TILES, 1, n_seq), seq_len, axis=2)
    seen = (row // seq_len == col // seq_len) & (col <= row) & (col % seq_len < lens)
    return seen.astype(F32)


def solution(mesh):
    act_spec = P('dp', None, None)
    w_specs = (P(None, None, 'tp', None), P(None, None, 'tp', None), P(None, None, 'tp', None),
               P(None, 'tp', None, None), P(None, None, 'tp'), P(None, 'tp', None))
    g_specs = (P('dp', None, 'tp', None), P('dp', None, 'tp', None), P('dp', None, 'tp', None),
               P('dp', 'tp', None, None), P('dp', None, 'tp'), P('dp', 'tp', None))

    def local_fn(y_one, y_two, dy_one, dy_two, seq_lens, w_query, w_key, w_value, w_out, w_up, w_down):
        n_batch, seq_len, width = y_one.shape
        tokens = n_batch * seq_len
        n_layers, _, n_heads, head_dim = w_query.shape
        slots = w_key.shape[2]
        flat = lambda val: val.reshape(tokens, width)
        norm = (y_one * lax.rsqrt(jnp.mean(y_one * y_one, axis=-1, keepdims=True) + EPS)).astype(BF16)
        tiled = lambda val: val.astype(BF16).reshape(N_TILES, 1, TILE, width)
        ne0 = jnp.concatenate([tiled(norm), tiled(dy_two)], axis=1)
        w_qkv = jnp.concatenate([w_val.reshape(n_layers, width, -1) for w_val in (w_query, w_key, w_value)], axis=2)
        state, n_g, e_g, h_all, u_all, n_f, e_f, a_all, dq, dk, dv = run_stack(
            ne0, tile_mask(seq_lens, seq_len), flat(y_one), flat(y_two), flat(dy_one), flat(dy_two),
            w_qkv, w_out.reshape(n_layers, n_heads * head_dim, width), w_up, w_down)

        def whole(val):
            blocks = lax.all_gather(val, 'tp', axis=0)
            return jnp.stack([blocks[owner] for owner in OWNER], axis=1).reshape(n_batch, seq_len, width)

        finals = tuple(whole(state[pos]) for pos in range(4))
        heads = lambda val, count: val.reshape(n_layers, tokens, count, head_dim)
        dot = functools.partial(jnp.einsum, preferred_element_type=F32)
        dw_query = dot('ltd,lthe->ldhe', n_f, heads(dq, n_heads))
        dw_key = dot('ltd,lthe->ldhe', n_f, heads(dk, slots))
        dw_value = dot('ltd,lthe->ldhe', n_f, heads(dv, slots))
        dw_out = dot('lthe,ltd->lhed', heads(a_all, n_heads), e_f)
        dw_up = dot('ltd,ltf->ldf', n_g, u_all)
        dw_down = dot('ltf,ltd->lfd', h_all, e_g)
        return finals + (dw_query, dw_key, dw_value, dw_out, dw_up, dw_down)

    return jax.shard_map(local_fn, mesh=mesh,
                         in_specs=(act_spec,) * 4 + (P('dp'),) + w_specs,
                         out_specs=(act_spec,) * 4 + g_specs,
                         check_vma=False)
```

time: 1330 us -> 825 us (0.62)
  waiting for transfers between devices: 789 us -> 36.7 us
  Pallas kernels: 0 us -> 587 us
  other arithmetic: 223 us -> 18 us
  matrix products: 281 us -> 76.8 us
  local copies, waits for them, and re-layouts: 16.8 us -> 90.4 us
    psum x6 -> x0, waiting for transfers between devices: 789 us -> none  [tp_sum(): return lax.psum(partial_val, 'tp')]
    pallas_call x0 -> x1, Pallas kernels: none -> 587 us  [run_stack(): pl.pallas_call(functools.partial(stack_kernel, n_layers, width, ff, qw, k...]
    dot_general x72 -> x6, matrix products: 281 us -> 76.8 us  [the longest x1 22.4 us: local_fn(): dw_down = dot('ltf,ltd->lfd', h_all, e_g)]
    another operation x9 -> x0, other arithmetic: 86.8 us -> none  [the longest x6 85.9 us: stack_grads(): jnp.stack([layer_grads[grad_pos] for layer_grads in grads_by_layer])]
    reduce_sum x15 -> x1, other arithmetic: 63.8 us -> 3.42 us  [local_fn(): jnp.mean(y_one * y_one, axis=-1, keepdims=True) + EPS]
    add x5 -> x1, other arithmetic: 60.3 us -> 0.01 us  [tile_mask(): col % seq_len < lens]
    unnamed x168 -> x59, local copies, waits for them, and re-layouts: 16.8 us -> 66.7 us
    all_gather x0 -> x4, waiting for transfers between devices: none -> 35 us  [whole(): blocks = lax.all_gather(val, 'tp', axis=0)]
  transfers between devices with their start and end apart: 6 -> 4, of which waited for: 6 -> 2; matrix products, arithmetic and copies ran while one was open for 13% -> 16% of each run, Pallas kernels for 0% -> 0%
where the time goes in v1:
time: 825 us; the launch traced here: 823 us
  Pallas kernels  587 us (71%)
  local copies, waits for them, and re-layouts  90.4 us (11%)
  matrix products  76.8 us (9%)
  waiting for transfers between devices  36.7 us (4%)
  other arithmetic  18 us (2%)
  between operations  14 us (2%)
    pallas_call x1, Pallas kernels, run_stack(): pl.pallas_call(functools.partial(stack_kernel, n_layers, width, ff, qw, k...  587 us
    unnamed x59, local copies, waits for them, and re-layouts  66.7 us
    all_gather x4, waiting for transfers between devices, whole(): blocks = lax.all_gather(val, 'tp', axis=0)  35 us
    dot_general x1, matrix products, local_fn(): dw_down = dot('ltf,ltd->lfd', h_all, e_g)  22.4 us
    dot_general x1, matrix products, local_fn(): dw_up = dot('ltd,ltf->ldf', n_g, u_all)  21.7 us
  transfers between devices with their start and end apart: 4, of which 2 were waited for; matrix products, arithmetic and copies ran while one was open for 16% of the time, Pallas kernels for 0%

profile of v1, /device:TPU:0, one launch (start us, length us, event | category | flops | bytes accessed | tf_op | source)
XLA Modules:
  0.0 822.7 jit_solution(13480750710806367366)
XLA Ops:
  8.2 10.3 %copy.47 = bf16[3,3072,3,128]{1,3,2,0:T(8,128)(2,1)} copy(bf16[3,3072,3,128]{3,1,2,0:T(8,128)(2,1)} %param.16) | data formatting | bytes 14155776 | tf_op args[5]
  18.4 10.4 %copy.48 = bf16[3,3072,384]{2,1,0:T(8,128)(2,1)} copy(bf16[3,3072,384]{1,2,0:T(8,128)(2,1)} %bitcast.175) | data formatting | bytes 14155776 | tf_op jit(solution)/shard_map/reshape | solution.py:358
  28.8 3.4 multiply_reduce_fusion
  34.7 2.1 convert_element_type.10
  36.8 5.6 pad_maximum_fusion.1.ne0
  42.9 5.1 pad_maximum_fusion.w_qkv
  48.8 586.5 %stack.17 = (f32[4,4,16,3072]{3,2,1,0:T(8,128)}, bf16[3,512,3072]{2,1,0:T(8,128)(2,1)}, bf16[3,512,3072]{2,1,0:T(8,128)(2,1)}, bf16[3,512,1024]{2,1,0:T(8,128)(2...) custom-call(bf16[4,2,128,3072]{3,2,1,0:T(8,128)(2,1)} %pad_maximum_f, ...), custom_call_target="tpu_custom_call" | custom-call | tf_op jit(solution)/shard_map/stack/pallas_call | solution.py:297
  635.4 3.7 fusion.39
  641.8 11.8 %fusion = f32[3,3072,3,128]{3,1,2,0:T(8,128)} fusion(bf16[3,512,3,128]{1,3,2,0:T(8,128)(2,1)S(1)} %bitcast.185, bf16[3,512,3072]{2,1,0:T(8,128)(2,1)} %get-tuple-element.22), kind=kOutput, calls=%fused_computation.1 | convolution fusion | flops 3623878656 | bytes 24772608 | tf_op jit(solution)/shard_map/ltd,lthe->ldhe/dot_general | solution.py:370
  653.7 5.0 fusion.40
  658.7 5.0 fusion.41
  664.3 21.7 %fusion.42 = f32[3,3072,1024]{2,1,0:T(8,128)} fusion(bf16[3,512,3072]{2,1,0:T(8,128)(2,1)} %get-tuple-element.28, bf16[3,512,1024]{2,1,0:T(8,128)(2,1)} %get-tuple-element.29), kind=kOutput, calls=%fused_computation.89 | convolution fusion | flops 9663676416 | bytes 50331648 | tf_op jit(solution)/shard_map/ltd,ltf->ldf/dot_general | solution.py:374
  686.0 22.4 %fusion.43 = f32[3,1024,3072]{2,1,0:T(8,128)} fusion(bf16[3,512,1024]{2,1,0:T(8,128)(2,1)} %get-tuple-element.30, bf16[3,512,3072]{2,1,0:T(8,128)(2,1)} %get-tuple-element.31), kind=kOutput, calls=%fused_computation.90 | convolution fusion | flops 9663676416 | bytes 50331648 | tf_op jit(solution)/shard_map/ltf,ltd->lfd/dot_general | solution.py:375
  708.4 11.0 %fusion.2 = f32[3,3,128,3072]{3,2,1,0:T(8,128)} fusion(bf16[3,512,3,128]{1,3,2,0:T(8,128)(2,1)S(1)} %bitcast.184, bf16[3,512,3072]{2,1,0:T(8,128)(2,1)} %get-tuple-element.27), kind=kOutput, calls=%fused_computation.3 | convolution fusion | flops 3623878656 | bytes 24772608 | tf_op jit(solution)/shard_map/lthe,ltd->lhed/dot_general | solution.py:373
  719.4 2.1 fusion.11
  721.4 2.1 fusion.10
  723.5 2.1 fusion.9
  725.6 2.1 fusion.8
  727.6 2.1 fusion.7
  729.7 2.1 fusion.6
  735.9 2.1 fusion.19
  752.5 9.7 %all-gather.7.cloned.1.call-done = f32[8,4,16,3072]{3,2,1,0:T(8,128)} async-done(((f32[1,4,16,3072]{3,2,1,0:T(8,128)}), f32[8,4,16,3072]{3,2,1,0:T(8,128)}) %all-gather.7.cloned.1.call-update) | async-done | bytes 6291472 | tf_op jit(solution)/shard_map/all_gather | solution.py:364
  778.7 25.3 %all-gather.5.cloned.1.call-done = f32[8,4,16,3072]{3,2,1,0:T(8,128)} async-done(((f32[1,4,16,3072]{3,2,1,0:T(8,128)}), f32[8,4,16,3072]{3,2,1,0:T(8,128)}) %all-gather.5.cloned.1.call-update) | async-done | bytes 6291472 | tf_op jit(solution)/shard_map/all_gather | solution.py:364
  813.5 2.7 copy-done.7
  (78 shorter events, 52.7 us)
Async XLA Ops:
  7.2 712.2 %all-gather.11.cloned.1.call-start = ((), (), s32[]{:S(2)}) async-start(), calls=%async_computation.3 | async-start | bytes 7077888 | tf_op jit(solution)/shard_map/all_gather | solution.py:364
  18.4 16.0 %slice-start.5 = ((s8[6291456]{0:T(1024)(128)(4,1)}), s8[2097152]{0:T(1024)(128)(4,1)S(1)}, s32[]{:S(2)}) async-start(s8[6291456]{0:T(1024)(128)(4,1)} %bitcast.177), calls=%async_computation.9 | async-start | bytes 4194304
  28.8 4.6 copy-start
  28.8 5.8 slice-start.6
  34.7 7.7 slice-start.3
  36.8 5.6 slice-start.4
  36.8 5.6 copy-start.1
  36.8 6.1 copy-start.2
  635.4 5.8 copy-start.4
  639.1 96.9 %all-gather.9.cloned.1.call-start = ((), (), s32[]{:S(2)}) async-start(), calls=%async_computation.2 | async-start | bytes 7077888 | tf_op jit(solution)/shard_map/all_gather | solution.py:364
  639.8 122.3 %all-gather.7.cloned.1.call-start = ((), (), s32[]{:S(2)}) async-start(), calls=%async_computation.1 | async-start | bytes 7077888 | tf_op jit(solution)/shard_map/all_gather | solution.py:364
  640.5 163.4 %all-gather.5.cloned.1.call-start = ((), (), s32[]{:S(2)}) async-start(), calls=%async_computation | async-start | bytes 7077888 | tf_op jit(solution)/shard_map/all_gather | solution.py:364
  641.1 12.5 %slice-start = ((s8[9437184]{0:T(1024)(128)(4,1)}), s8[1048576]{0:T(1024)(128)(4,1)S(1)}, s32[]{:S(2)}) async-start(s8[9437184]{0:T(1024)(128)(4,1)} %bitcast.170), calls=%async_computation.4 | async-start | bytes 2097152
  641.8 11.8 %slice-start.1 = ((s8[9437184]{0:T(1024)(128)(4,1)}), s8[4194304]{0:T(1024)(128)(4,1)S(1)}, s32[]{:S(2)}) async-start(s8[9437184]{0:T(1024)(128)(4,1)} %bitcast.170), calls=%async_computation.5 | async-start | bytes 8388608
  641.8 11.8 %slice-start.2 = ((s8[9437184]{0:T(1024)(128)(4,1)}), s8[4194304]{0:T(1024)(128)(4,1)S(1)}, s32[]{:S(2)}) async-start(s8[9437184]{0:T(1024)(128)(4,1)} %bitcast.170), calls=%async_computation.6 | async-start | bytes 8388608
  641.8 11.8 %copy-start.6 = (bf16[3,512,128]{2,1,0:T(8,128)(2,1)S(1)}, bf16[3,512,128]{2,1,0:T(8,128)(2,1)}, u32[]{:S(2)}) copy-start(bf16[3,512,128]{2,1,0:T(8,128)(2,1)} %get-tuple-element.24) | copy-start | bytes 1179652
  653.6 5.0 copy-start.5
  658.7 5.0 copy-start.3
  813.5 2.7 copy-start.7
Sparse Core Ops, SparseCore 0:
  639.2 39.0 all-gather.10
  680.6 39.5 all-gather.8
  722.6 39.5 all-gather.6
  764.4 39.5 all-gather.4

commit v2 on v1

--- a/solution.py
+++ b/solution.py
@@ -16,8 +16,7 @@
 N_TILES = 4
 GELU_C = 0.7978845608028654
 GELU_A = 0.044715
-OWNER = (0, 4, 2, 6, 1, 3, 5, 7)
-ORDER = (('e', 3), ('g', 4), ('C', 0), ('f', 3), ('b', 0), ('c', 1), ('d', 2))
+ORDER = (('g', 4), ('C', 0), ('e', 3), ('c', 1), ('b', 0), ('f', 3), ('d', 2))
 
 
 def dot_nn(lhs, rhs):
@@ -37,10 +36,10 @@
 
 
 def stack_kernel(n_layers, width, ff, qw, kw,
-                 ne0, mask, y_one, y_two, dy_one, dy_two, w_qkv, w_out, w_up, w_down,
-                 o_state, o_ng, o_eg, o_h, o_u, o_nf, o_ef, o_a, o_dq, o_dk, o_dv,
-                 ne, part, rec_d, rec_one, rec_two, x_st, d_st, wu, wd, wqkv, wo, h_buf, u_buf,
-                 a_buf, dqkv_buf, q_buf, send_sem, recv_sem, w_sem, in_sem, out_sem):
+                 mask, y_one, y_two, dy_one, dy_two, w_query, w_key, w_value, w_out, w_up, w_down,
+                 o_x1, o_dx2, o_x2, o_dy1, o_ng, o_eg, o_h, o_u, o_nf, o_ef, o_a, o_dq, o_dk, o_dv,
+                 ne_bf, part, rec_d, rec_one, rec_two, x_st, d_st, wu, wd, wqkv, wo, h_buf, u_buf,
+                 a_buf, dqkv_buf, q_buf, send_sem, recv_sem, w_sem, in_sem, act_sem, out_sem, free_sem):
     n_steps = 2 * n_layers * N_TILES
     me = lax.axis_index('tp')
     core = me % 2
@@ -65,19 +64,32 @@
                 pltpu.make_async_copy(w_down.at[layer], wd, w_sem.at[1]))
 
     def attn_loads(layer):
-        return (pltpu.make_async_copy(w_qkv.at[layer], wqkv, w_sem.at[2]),
-                pltpu.make_async_copy(w_out.at[layer], wo, w_sem.at[3]))
-
-    in_copies = [pltpu.make_async_copy(ne0, ne, in_sem.at[0])]
-    for pos, (src, dst) in enumerate(((y_one, x_st.at[0]), (y_two, x_st.at[1]),
-                                      (dy_one, d_st.at[0]), (dy_two, d_st.at[1]))):
-        for tile in range(N_TILES):
-            in_copies.append(pltpu.make_async_copy(
-                src.at[pl.ds(tile * TILE + own, 16), :], dst.at[tile], in_sem.at[1 + pos * N_TILES + tile]))
+        heads = [w_query.at[layer, head] for head in range(qw // kw)]
+        heads += [w_key.at[layer, 0], w_value.at[layer, 0]]
+        copies = [pltpu.make_async_copy(src, wqkv.at[:, pl.ds(pos * kw, kw)], w_sem.at[3 + pos])
+                  for pos, src in enumerate(heads)]
+        return copies + [pltpu.make_async_copy(w_out.at[layer], wo, w_sem.at[2])]
+
+    def act_loads(tile):
+        rows = pl.ds(tile * TILE, TILE)
+        return (pltpu.make_async_copy(y_one.at[rows, :], part.at[tile, 0], act_sem.at[tile, 0]),
+                pltpu.make_async_copy(dy_two.at[rows, :], part.at[tile, 1], act_sem.at[tile, 1]))
+
+    def own_loads(tile):
+        pairs = ((y_one, x_st.at[0]), (y_two, x_st.at[1]), (dy_one, d_st.at[0]), (dy_two, d_st.at[1]))
+        return [pltpu.make_async_copy(src.at[pl.ds(tile * TILE + own, 16), :], dst.at[tile], in_sem.at[pos, tile])
+                for pos, (src, dst) in enumerate(pairs)]
+
+    for copy in act_loads(0):
+        copy.start()
     for copy in mlp_loads(n_layers - 1):
         copy.start()
-    for copy in in_copies:
-        copy.start()
+    for tile in range(1, N_TILES):
+        for copy in act_loads(tile):
+            copy.start()
+    for tile in range(N_TILES):
+        for copy in own_loads(tile):
+            copy.start()
     for copy in attn_loads(n_layers - 1):
         copy.start()
 
@@ -85,10 +97,9 @@
     for peer in (mate, x_peer, y_peer):
         pl.semaphore_signal(barrier, inc=1, device_id={'tp': peer}, device_id_type=MESH)
     pl.semaphore_wait(barrier, 3)
-    for copy in in_copies:
-        copy.wait()
-
-    def remote(stage, tile):
+
+    def remote(stage, tile, wide=False):
+        ne = part if wide else ne_bf
         src, dst, peer = {
             0: lambda: (part.at[tile, :, pl.ds(half_other, 64), :], rec_d.at[tile], mate),
             1: lambda: (part.at[tile, :, pl.ds(quarter_other, 32), :], rec_one.at[tile], peer_one),
@@ -101,7 +112,24 @@
             src_ref=src, dst_ref=dst, send_sem=send_sem.at[tile, stage], recv_sem=recv_sem.at[tile, stage],
             device_id={'tp': peer}, device_id_type=MESH)
 
+    ne = ne_bf
+
+    def convert(tile):
+        @pl.loop(0, TILE // 16)
+        def _(pos):
+            rows = pl.ds(pl.multiple_of(pos * 16, 16), 16)
+            x_val = part[tile, 0, rows, :]
+            ne[tile, 0, rows, :] = (x_val * inv_rms_of(x_val)).astype(BF16)
+            ne[tile, 1, rows, :] = part[tile, 1, rows, :].astype(BF16)
+
     def mlp_tile(layer, tile):
+        @pl.when(layer == n_layers - 1)
+        def _():
+            for copy in act_loads(tile):
+                copy.wait()
+            convert(tile)
+
+
         rows = pl.ds(tile * TILE, TILE)
         saves = [pltpu.make_async_copy(ne.at[tile, 0], o_ng.at[layer, rows, :], out_sem.at[0]),
                  pltpu.make_async_copy(ne.at[tile, 1], o_eg.at[layer, rows, :], out_sem.at[1])]
@@ -144,6 +172,15 @@
 
     def attn_tile(layer, tile):
         rows = pl.ds(tile * TILE, TILE)
+        wide_saves = [pltpu.make_async_copy(part.at[tile, 0], o_x2.at[rows, :], out_sem.at[6]),
+                      pltpu.make_async_copy(part.at[tile, 1], o_dy1.at[rows, :], out_sem.at[7])]
+
+        @pl.when(layer == 0)
+        def _():
+            for copy in wide_saves:
+                copy.start()
+            convert(tile)
+
         saves = [pltpu.make_async_copy(ne.at[tile, 0], o_nf.at[layer, rows, :], out_sem.at[0]),
                  pltpu.make_async_copy(ne.at[tile, 1], o_ef.at[layer, rows, :], out_sem.at[1])]
         for copy in saves:
@@ -188,6 +225,11 @@
         for copy in more:
             copy.start()
 
+        @pl.when(layer == 0)
+        def _():
+            for copy in wide_saves:
+                copy.wait()
+
         @pl.loop(0, width // 512)
         def _(pos):
             cols = pl.ds(pl.multiple_of(pos * 512, 512), 512)
@@ -210,26 +252,53 @@
                 dst = pl.ds(pl.multiple_of(base + row, 8), 8)
                 part[tile, unit, dst, :] += received[tile, unit, pl.ds(row, 8), :]
 
-    def finish_rows(branch, tile):
+    def finish_rows(branch, tile, wide):
         rows = pl.ds(own, 16)
         other = 1 - branch
         x_new = x_st[other, tile] - (part[tile, 0, rows, :] + rec_two[tile, 0])
         x_st[other, tile] = x_new
-        ne[tile, 0, rows, :] = (x_new * inv_rms_of(x_new)).astype(BF16)
         grad = part[tile, 1, rows, :] + rec_two[tile, 1]
         x_val = x_st[branch, tile]
         inv = inv_rms_of(x_val)
         normed = x_val * inv
         d_new = d_st[branch, tile] + inv * (grad - normed * jnp.mean(grad * normed, axis=-1, keepdims=True))
         d_st[branch, tile] = d_new
-        ne[tile, 1, rows, :] = d_new.astype(BF16)
+
+        @pl.when(wide)
+        def _():
+            part[tile, 0, rows, :] = x_new
+            part[tile, 1, rows, :] = d_new
+
+        @pl.when(jnp.logical_not(wide))
+        def _():
+            ne[tile, 0, rows, :] = (x_new * inv_rms_of(x_new)).astype(BF16)
+            ne[tile, 1, rows, :] = d_new.astype(BF16)
 
     def run_stage(stage, idx):
         tile = idx % N_TILES
         turn = idx // N_TILES
         branch = turn % 2
         layer = n_layers - 1 - turn // 2
-        travels = idx < n_steps - N_TILES
+        last = n_steps - N_TILES
+        wide = (idx >= last - N_TILES) & (idx < last)
+        narrow = idx < last - N_TILES
+
+        def gather(waits, starts):
+            for is_wide, cond in ((True, wide), (False, narrow)):
+                @pl.when(cond)
+                def _():
+                    if waits is not None:
+                        remote(waits, tile, is_wide).wait()
+                    if starts is not None:
+                        if is_wide:
+                            pl.semaphore_wait(free_sem.at[tile, starts - 3], 1)
+                        remote(starts, tile, is_wide).start()
+
+        def release(slot, peer):
+            @pl.when(wide)
+            def _():
+                pl.semaphore_signal(free_sem.at[tile, slot], inc=1, device_id={'tp': peer}, device_id_type=MESH)
+
         if stage == 'C':
             @pl.when(branch == 0)
             def _():
@@ -241,33 +310,30 @@
             remote(0, tile).start()
         elif stage == 'b':
             remote(0, tile).wait()
+            release(2, mate)
             add_rows(tile, half, 64, rec_d)
             remote(1, tile).start()
         elif stage == 'c':
             remote(1, tile).wait()
+            release(1, peer_one)
             add_rows(tile, quarter, 32, rec_one)
             remote(2, tile).start()
         elif stage == 'd':
             remote(2, tile).wait()
-            finish_rows(branch, tile)
-
-            @pl.when(travels)
+            release(0, peer_two)
+
+            @pl.when(turn == 0)
             def _():
-                remote(3, tile).start()
+                for copy in own_loads(tile):
+                    copy.wait()
+            finish_rows(branch, tile, wide)
+            gather(None, 3)
         elif stage == 'e':
-            @pl.when(travels)
-            def _():
-                remote(3, tile).wait()
-                remote(4, tile).start()
+            gather(3, 4)
         elif stage == 'f':
-            @pl.when(travels)
-            def _():
-                remote(4, tile).wait()
-                remote(5, tile).start()
+            gather(4, 5)
         else:
-            @pl.when(travels)
-            def _():
-                remote(5, tile).wait()
+            gather(5, None)
 
     max_lag = max(lag for _, lag in ORDER)
 
@@ -278,29 +344,30 @@
             def _():
                 run_stage(stage, step - lag)
 
-    finals = []
-    for pos, src in enumerate((x_st.at[0], x_st.at[1], d_st.at[0], d_st.at[1])):
-        finals.append(pltpu.make_async_copy(src, o_state.at[pos], out_sem.at[pos]))
+    finals = [pltpu.make_async_copy(x_st.at[0], o_x1, out_sem.at[0]),
+              pltpu.make_async_copy(d_st.at[1], o_dx2, out_sem.at[1])]
     for copy in finals:
         copy.start()
     for copy in finals:
         copy.wait()
 
 
-def run_stack(ne0, mask, y_one, y_two, dy_one, dy_two, w_qkv, w_out, w_up, w_down):
+def run_stack(mask, y_one, y_two, dy_one, dy_two, w_query, w_key, w_value, w_out, w_up, w_down):
     n_layers, width, ff = w_up.shape
     qw = w_out.shape[1]
-    kw = (w_qkv.shape[2] - qw) // 2
+    kw = w_key.shape[3]
     tokens = y_one.shape[0]
     any_spec = pl.BlockSpec(memory_space=pl.ANY)
     out = lambda *shape: jax.ShapeDtypeStruct((n_layers, tokens) + shape, BF16)
+    rows = jax.ShapeDtypeStruct((N_TILES, 16, width), F32)
+    full = jax.ShapeDtypeStruct((tokens, width), F32)
     return pl.pallas_call(
         functools.partial(stack_kernel, n_layers, width, ff, qw, kw),
-        out_shape=(jax.ShapeDtypeStruct((4, N_TILES, 16, width), F32),
+        out_shape=(rows, rows, full, full,
                    out(width), out(width), out(ff), out(ff), out(width), out(width),
                    out(qw), out(qw), out(kw), out(kw)),
-        in_specs=[any_spec, pl.BlockSpec(memory_space=pltpu.VMEM)] + [any_spec] * 8,
-        out_specs=(any_spec,) * 11,
+        in_specs=[pl.BlockSpec(memory_space=pltpu.VMEM)] + [any_spec] * 10,
+        out_specs=(any_spec,) * 14,
         scratch_shapes=[
             pltpu.VMEM((N_TILES, 2, TILE, width), BF16),
             pltpu.VMEM((N_TILES, 2, TILE, width), F32),
@@ -320,14 +387,38 @@
             pltpu.VMEM((TILE, qw + 2 * kw), BF16),
             pltpu.SemaphoreType.DMA((N_TILES, 6)),
             pltpu.SemaphoreType.DMA((N_TILES, 6)),
-            pltpu.SemaphoreType.DMA((4,)),
-            pltpu.SemaphoreType.DMA((1 + 4 * N_TILES,)),
-            pltpu.SemaphoreType.DMA((6,)),
+            pltpu.SemaphoreType.DMA((5 + qw // kw,)),
+            pltpu.SemaphoreType.DMA((4, N_TILES)),
+            pltpu.SemaphoreType.DMA((N_TILES, 2)),
+            pltpu.SemaphoreType.DMA((8,)),
+            pltpu.SemaphoreType.REGULAR((N_TILES, 3)),
         ],
         compiler_params=pltpu.CompilerParams(
             collective_id=0, has_side_effects=True, vmem_limit_bytes=67043328),
         name='stack',
-    )(ne0, mask, y_one, y_two, dy_one, dy_two, w_qkv, w_out, w_up, w_down)
+    )(mask, y_one, y_two, dy_one, dy_two, w_query, w_key, w_value, w_out, w_up, w_down)
+
+
+def order_rows(blocks):
+    n_dev, n_tiles, n_rows, width = blocks.shape
+
+    def source(pos):
+        core, first, second = pos // 4, (pos // 2) % 2, pos % 2
+        return core + (1 - core) * (4 * second + 2 * first) + core * (4 * first + 2 * second)
+
+    def body(src, dst):
+        for tile in range(n_tiles):
+            dst[tile, 0] = src[0, tile]
+
+    return pl.pallas_call(
+        body,
+        grid=(n_dev,),
+        out_shape=jax.ShapeDtypeStruct((n_tiles, n_dev, n_rows, width), blocks.dtype),
+        in_specs=[pl.BlockSpec((1, n_tiles, n_rows, width), lambda pos: (source(pos), 0, 0, 0))],
+        out_specs=pl.BlockSpec((n_tiles, 1, n_rows, width), lambda pos: (0, pos, 0, 0)),
+        cost_estimate=pl.CostEstimate(flops=10 ** 8, bytes_accessed=2 * blocks.size * 4, transcendentals=0),
+        name='order_rows',
+    )(blocks)
 
 
 def tile_mask(seq_lens, seq_len):
@@ -352,19 +443,14 @@
         n_layers, _, n_heads, head_dim = w_query.shape
         slots = w_key.shape[2]
         flat = lambda val: val.reshape(tokens, width)
-        norm = (y_one * lax.rsqrt(jnp.mean(y_one * y_one, axis=-1, keepdims=True) + EPS)).astype(BF16)
-        tiled = lambda val: val.astype(BF16).reshape(N_TILES, 1, TILE, width)
-        ne0 = jnp.concatenate([tiled(norm), tiled(dy_two)], axis=1)
-        w_qkv = jnp.concatenate([w_val.reshape(n_layers, width, -1) for w_val in (w_query, w_key, w_value)], axis=2)
-        state, n_g, e_g, h_all, u_all, n_f, e_f, a_all, dq, dk, dv = run_stack(
-            ne0, tile_mask(seq_lens, seq_len), flat(y_one), flat(y_two), flat(dy_one), flat(dy_two),
-            w_qkv, w_out.reshape(n_layers, n_heads * head_dim, width), w_up, w_down)
-
-        def whole(val):
-            blocks = lax.all_gather(val, 'tp', axis=0)
-            return jnp.stack([blocks[owner] for owner in OWNER], axis=1).reshape(n_batch, seq_len, width)
-
-        finals = tuple(whole(state[pos]) for pos in range(4))
+        by_head = lambda val: jnp.transpose(val, (0, 2, 1, 3))
+        x_one, dx_two, x_two, dx_one, n_g, e_g, h_all, u_all, n_f, e_f, a_all, dq, dk, dv = run_stack(
+            tile_mask(seq_lens, seq_len), flat(y_one), flat(y_two), flat(dy_one), flat(dy_two),
+            by_head(w_query), by_head(w_key), by_head(w_value),
+            w_out.reshape(n_layers, n_heads * head_dim, width), w_up, w_down)
+        shape = lambda val: val.reshape(n_batch, seq_len, width)
+        whole = lambda val: shape(order_rows(lax.all_gather(val, 'tp', axis=0)))
+        finals = (whole(x_one), shape(x_two), shape(dx_one), whole(dx_two))
         heads = lambda val, count: val.reshape(n_layers, tokens, count, head_dim)
         dot = functools.partial(jnp.einsum, preferred_element_type=F32)
         dw_query = dot('ltd,lthe->ldhe', n_f, heads(dq, n_heads))

time: 825 us -> 620 us (0.75)
  local copies, waits for them, and re-layouts: 90.4 us -> 13.2 us
  Pallas kernels: 587 us -> 510 us
  waiting for transfers between devices: 36.7 us -> 0.72 us
  other arithmetic: 18 us -> 0.85 us
    pallas_call x1, Pallas kernels: 587 us -> 494 us  [run_stack(): pl.pallas_call(functools.partial(stack_kernel, n_layers, width, ff, qw, k...]
    unnamed x59 -> x12, local copies, waits for them, and re-layouts: 66.7 us -> 9.11 us
    all_gather x4 -> x2, waiting for transfers between devices: 35 us -> 0.01 us  [local_fn(): whole = lambda val: shape(order_rows(lax.all_gather(val, 'tp', axis=0)))]
    pallas_call x0 -> x2, Pallas kernels: none -> 15.8 us  [order_rows(): pl.pallas_call(body, grid=(n_dev,), out_shape=jax.ShapeDtypeStruct((n_til...]
    concatenate x2 -> x0, other arithmetic: 10.6 us -> none  [the longest x1 5.57 us: local_fn(): ne0 = jnp.concatenate([tiled(norm), tiled(dy_two)], axis=1)]
    reshape x1 -> x0, local copies, waits for them, and re-layouts: 10.4 us -> none  [local_fn(): w_val.reshape(n_layers, width, -1)]
  transfers between devices with their start and end apart: 4 -> 2, of which waited for: 2 -> 0; matrix products, arithmetic and copies ran while one was open for 16% -> 14% of each run, Pallas kernels for 0% -> 1%
where the time goes in v2:
time: 620 us
  Pallas kernels  510 us (82%)
  matrix products  80.9 us (13%)
  between operations  14.1 us (2%)
  local copies, waits for them, and re-layouts  13.2 us (2%)
    pallas_call x1, Pallas kernels, run_stack(): pl.pallas_call(functools.partial(stack_kernel, n_layers, width, ff, qw, k...  494 us
    dot_general x1, matrix products, local_fn(): dw_down = dot('ltf,ltd->lfd', h_all, e_g)  22.4 us
    dot_general x1, matrix products, local_fn(): dw_up = dot('ltd,ltf->ldf', n_g, u_all)  21.5 us
    pallas_call x2, Pallas kernels, order_rows(): pl.pallas_call(body, grid=(n_dev,), out_shape=jax.ShapeDtypeStruct((n_til...  15.8 us
  transfers between devices with their start and end apart: 2, of which 0 were waited for; matrix products, arithmetic and copies ran while one was open for 14% of the time, Pallas kernels for 1%

profile of v2, /device:TPU:0, one launch (start us, length us, event | category | flops | bytes accessed | tf_op | source)
XLA Modules:
  0.0 619.8 jit_solution(15017724311667470041)
XLA Ops:
  7.2 0.0 all-gather.7.cloned.1.call-start
  7.3 0.7 reshape.70
  8.0 0.1 broadcast_in_dim.5
  8.1 0.1 broadcast_in_dim.6
  8.2 0.8 fusion.6.mask
  9.0 494.2 %stack.1 = (f32[4,16,3072]{2,1,0:T(8,128)}, f32[4,16,3072]{2,1,0:T(8,128)}, f32[512,3072]{1,0:T(8,128)}, f32[512,3072]{1,0:T(8,128)}, bf16[3,512,3072]{2,1,0:T(8...) custom-call(f32[4,128,128]{2,1,0:T(8,128)} %fusion.6.mask, ...), custom_call_target="tpu_custom_call" | custom-call | tf_op jit(solution)/shard_map/stack/pallas_call | solution.py:364
  503.2 0.0 all-gather.7.cloned.1.call-update
  503.3 0.0 all-gather.5.cloned.1.call-start
  503.3 0.7 all-gather.5.cloned.1.call-update
  504.0 1.6 copy.40
  505.6 1.6 copy.45
  507.2 0.0 copy-done.2
  507.2 0.0 copy-start
  507.2 0.0 copy-start.1
  507.2 9.4 %fusion.8 = f32[3,3072,128]{2,1,0:T(8,128)} fusion(bf16[3,512,3072]{2,1,0:T(8,128)(2,1)} %get-tuple-element.28, bf16[3,512,128]{2,1,0:T(8,128)(2,1)S(1)} %copy-done.2), kind=kOutput, calls=%fused_computation.18 | convolution fusion | flops 1207959552 | bytes 14548992 | tf_op jit(solution)/shard_map/ltd,lthe->ldhe/dot_general | solution.py:458
  516.6 5.0 fusion.7
  521.6 11.0 %fusion.2 = f32[3,3,128,3072]{3,2,1,0:T(8,128)} fusion(bf16[3,512,3,128]{1,3,2,0:T(8,128)(2,1)S(1)} %bitcast.57, bf16[3,512,3072]{2,1,0:T(8,128)(2,1)} %get-tuple-element.33), kind=kOutput, calls=%fused_computation.2 | convolution fusion | flops 3623878656 | bytes 24772608 | tf_op jit(solution)/shard_map/lthe,ltd->lhed/dot_general | solution.py:459
  532.6 22.4 %fusion.10 = f32[3,1024,3072]{2,1,0:T(8,128)} fusion(bf16[3,512,1024]{2,1,0:T(8,128)(2,1)} %get-tuple-element.36, bf16[3,512,3072]{2,1,0:T(8,128)(2,1)} %get-tuple-element.37), kind=kOutput, calls=%fused_computation.20 | convolution fusion | flops 9663676416 | bytes 50331648 | tf_op jit(solution)/shard_map/ltf,ltd->lfd/dot_general | solution.py:461
  555.0 21.5 %fusion.9 = f32[3,3072,1024]{2,1,0:T(8,128)} fusion(bf16[3,512,3072]{2,1,0:T(8,128)(2,1)} %get-tuple-element.34, bf16[3,512,1024]{2,1,0:T(8,128)(2,1)} %get-tuple-element.35), kind=kOutput, calls=%fused_computation.19 | convolution fusion | flops 9663676416 | bytes 50331648 | tf_op jit(solution)/shard_map/ltd,ltf->ldf/dot_general | solution.py:460
  576.5 11.6 %fusion = f32[3,3072,3,128]{3,1,2,0:T(8,128)} fusion(bf16[3,512,3,128]{1,3,2,0:T(8,128)(2,1)S(1)} %bitcast.56, bf16[3,512,3072]{2,1,0:T(8,128)(2,1)} %get-tuple-element.28), kind=kOutput, calls=%fused_computation | convolution fusion | flops 3623878656 | bytes 24772608 | tf_op jit(solution)/shard_map/ltd,lthe->ldhe/dot_general | solution.py:456
  588.1 7.8 %order_rows.3 = f32[4,8,16,3072]{3,2,1,0:T(8,128)} custom-call(f32[8,4,16,3072]{3,2,1,0:T(8,128)} %bitcast.52), custom_call_target="tpu_custom_call" | custom-call | flops 100000000 | bytes 12582912 | tf_op jit(solution)/shard_map/order_rows/pallas_call | solution.py:413
  595.9 8.0 %order_rows.2 = f32[4,8,16,3072]{3,2,1,0:T(8,128)} custom-call(f32[8,4,16,3072]{3,2,1,0:T(8,128)} %bitcast.53), custom_call_target="tpu_custom_call" | custom-call | flops 100000000 | bytes 12582912 | tf_op jit(solution)/shard_map/order_rows/pallas_call | solution.py:413
  603.9 6.4 %copy.61 = f32[16,32,3072]{2,1,0:T(8,128)} copy(f32[16,32,3072]{2,1,0:T(8,128)} %bitcast.51) | data formatting | bytes 12582912
  610.3 2.7 copy.62
  (13 shorter events, 0.0 us)
Async XLA Ops:
  7.2 580.9 %all-gather.7.cloned.1.call-start = ((), (), s32[]{:S(2)}) async-start(), calls=%async_computation.1 | async-start | bytes 7077888 | tf_op jit(solution)/shard_map/all_gather | solution.py:452
  503.2 4.0 copy-start.2
  503.3 92.7 %all-gather.5.cloned.1.call-start = ((), (), s32[]{:S(2)}) async-start(), calls=%async_computation | async-start | bytes 7077888 | tf_op jit(solution)/shard_map/all_gather | solution.py:452
  507.2 9.4 %copy-start = (bf16[3,512,3072]{2,1,0:T(8,128)(2,1)S(1)}, bf16[3,512,3072]{2,1,0:T(8,128)(2,1)}, u32[]{:S(2)}) copy-start(bf16[3,512,3072]{2,1,0:T(8,128)(2,1)} %get-tuple-element.28) | copy-start | bytes 28311556
  507.2 9.4 %copy-start.1 = (bf16[3,512,128]{2,1,0:T(8,128)(2,1)S(1)}, bf16[3,512,128]{2,1,0:T(8,128)(2,1)}, u32[]{:S(2)}) copy-start(bf16[3,512,128]{2,1,0:T(8,128)(2,1)} %get-tuple-element.30) | copy-start | bytes 1179652
  595.9 14.4 %slice-start = ((s8[6291456]{0:T(1024)(128)(4,1)}), s8[2097152]{0:T(1024)(128)(4,1)S(1)}, s32[]{:S(2)}) async-start(s8[6291456]{0:T(1024)(128)(4,1)} %bitcast.48), calls=%async_computation.2 | async-start | bytes 4194304
  603.9 6.4 %slice-start.1 = ((s8[6291456]{0:T(1024)(128)(4,1)}), s8[4194304]{0:T(1024)(128)(4,1)S(1)}, s32[]{:S(2)}) async-start(s8[6291456]{0:T(1024)(128)(4,1)} %bitcast.48), calls=%async_computation.3 | async-start | bytes 8388608
Sparse Core Ops, SparseCore 0:
  503.4 39.0 all-gather.6
  544.2 39.5 all-gather.4
